TPU v7x, 32 devices: a whole 2x2x4 slice. The times are simulated.
32 devices in a mesh: shift: 2 (over x), batch: 4 (over z), cols: 4 (over y, core).
Axes of the slice: x: 2, y: 2, z: 4, core: 2. Of those that a mesh axis runs over, the one named last changes fastest.
Arguments:
- partial_up: float32 [8, 768, 3072], P(('shift', 'batch'), None, 'cols'), parts along dimension 0, may hold values from -0.875 to 0.875
- partial_down: float32 [8, 3072, 768], P(('shift', 'batch'), 'cols'), parts along dimension 0, may hold values from -0.875 to 0.875
- partial_norm: float32 [8, 768], P(('shift', 'batch')), parts along dimension 0, may hold values from -8 to 8
- partial_bias: float32 [8, 768], P(('shift', 'batch')), parts along dimension 0, may hold values from -8 to 8
- master_up: float32 [1536, 3072], P(('shift', 'batch'), 'cols'), parts along dimension 0, may hold values from -0.21875 to 0.21875
- master_down: float32 [6144, 768], P(('shift', 'cols'), 'batch'), parts along dimension 0, may hold values from -0.109375 to 0.109375
- master_norm: float32 [1536], P(('shift', 'batch')), parts along dimension 0, may hold values from 0.25 to 1.75
- master_bias: float32 [1536], P(('shift', 'batch')), parts along dimension 0, may hold values from -3 to 3
- memory_up: float32 [1536, 3072], P(('shift', 'batch'), 'cols'), parts along dimension 0, may hold values from -1.75 to 1.75
- memory_down: float32 [6144, 768], P(('shift', 'cols'), 'batch'), parts along dimension 0, may hold values from -1.75 to 1.75
- memory_norm: float32 [1536], P(('shift', 'batch')), parts along dimension 0, may hold values from -1.75 to 1.75
- memory_bias: float32 [1536], P(('shift', 'batch')), parts along dimension 0, may hold values from -1.75 to 1.75
Outputs:
- compute_up: bfloat16 [1536, 3072], P('shift', 'cols'), parts along dimension 0
- compute_down: bfloat16 [6144, 768], P(('shift', 'cols')), parts along dimension 0
- compute_norm: bfloat16 [1536], P('shift'), parts along dimension 0
- compute_bias: bfloat16 [1536], P('shift'), parts along dimension 0
- stepped_up: float32 [1536, 3072], P(('shift', 'batch'), 'cols'), parts along dimension 0
- stepped_down: float32 [6144, 768], P(('shift', 'cols'), 'batch'), parts along dimension 0
- stepped_norm: float32 [1536], P(('shift', 'batch')), parts along dimension 0
- stepped_bias: float32 [1536], P(('shift', 'batch')), parts along dimension 0
- state_new_up: float32 [1536, 3072], P(('shift', 'batch'), 'cols'), parts along dimension 0
- state_new_down: float32 [6144, 768], P(('shift', 'cols'), 'batch'), parts along dimension 0
- state_new_norm: float32 [1536], P(('shift', 'batch')), parts along dimension 0
- state_new_bias: float32 [1536], P(('shift', 'batch')), parts along dimension 0
There are 2 independent parts, one for each index of `shift`. A program takes and returns all parts, laid end to end along the dimension named above; each array names one. Nothing has to cross between parts.
All inputs are finite; a program needn't handle non-finite values.
Results may differ from a plain program's by a relative error of at most 0.0085.
Values may be sent and summed in bfloat16 or wider, within the bound.
A program may use at most 64 MiB of HBM per device.

v0:
```python
import jax
import jax.numpy as jnp
from jax import lax
from jax.sharding import PartitionSpec as P

learn_rate = 0.1
hold_rate = 0.8


def on_device(
    partial_up,
    partial_down,
    partial_norm,
    partial_bias,
    master_up,
    master_down,
    master_norm,
    master_bias,
    memory_up,
    memory_down,
    memory_norm,
    memory_bias,
):
    mean_up, mean_down = (
        lax.psum_scatter(
            partial_up[0].astype(jnp.bfloat16), "batch", scatter_dimension=0, tiled=True
        ).astype(jnp.float32),
        lax.psum_scatter(
            partial_down[0].astype(jnp.bfloat16), "batch", scatter_dimension=1, tiled=True
        ).astype(jnp.float32),
    )
    whole_norm, whole_bias = lax.psum((partial_norm[0], partial_bias[0]), "batch")
    place = lax.axis_index("batch")
    mean_norm = lax.dynamic_slice_in_dim(
        whole_norm, place * master_norm.shape[0], master_norm.shape[0]
    )
    mean_bias = lax.dynamic_slice_in_dim(
        whole_bias, place * master_bias.shape[0], master_bias.shape[0]
    )
    mean_rate = lax.axis_size("batch") ** (-0.5)
    mean_up = mean_up * mean_rate
    mean_down = mean_down * mean_rate
    mean_norm = mean_norm * mean_rate
    mean_bias = mean_bias * mean_rate
    state_new_up = hold_rate * memory_up + mean_up
    stepped_up = master_up - learn_rate * state_new_up
    state_new_down = hold_rate * memory_down + mean_down
    stepped_down = master_down - learn_rate * state_new_down
    state_new_norm = hold_rate * memory_norm + mean_norm
    stepped_norm = master_norm - learn_rate * state_new_norm
    state_new_bias = hold_rate * memory_bias + mean_bias
    stepped_bias = master_bias - learn_rate * state_new_bias
    compute_up, compute_down, compute_norm, compute_bias = (
        lax.all_gather(stepped_up.astype(jnp.bfloat16), "batch", axis=0, tiled=True),
        lax.all_gather(stepped_down.astype(jnp.bfloat16), "batch", axis=1, tiled=True),
        lax.all_gather(stepped_norm.astype(jnp.bfloat16), "batch", axis=0, tiled=True),
        lax.all_gather(stepped_bias.astype(jnp.bfloat16), "batch", axis=0, tiled=True),
    )
    return (
        compute_up,
        compute_down,
        compute_norm,
        compute_bias,
        stepped_up,
        stepped_down,
        stepped_norm,
        stepped_bias,
        state_new_up,
        state_new_down,
        state_new_norm,
        state_new_bias,
    )


def solution(mesh):
    return jax.shard_map(
        on_device,
        mesh=mesh,
        in_specs=(
            P(("shift", "batch"), None, "cols"),
            P(("shift", "batch"), "cols", None),
            P(("shift", "batch"), None),
            P(("shift", "batch"), None),
            P(("shift", "batch"), "cols"),
            P(("shift", "cols"), "batch"),
            P(("shift", "batch")),
            P(("shift", "batch")),
            P(("shift", "batch"), "cols"),
            P(("shift", "cols"), "batch"),
            P(("shift", "batch")),
            P(("shift", "batch")),
        ),
        out_specs=(
            P("shift", "cols"),
            P(("shift", "cols"), None),
            P("shift"),
            P("shift"),
            P(("shift", "batch"), "cols"),
            P(("shift", "cols"), "batch"),
            P(("shift", "batch")),
            P(("shift", "batch")),
            P(("shift", "batch"), "cols"),
            P(("shift", "cols"), "batch"),
            P(("shift", "batch")),
            P(("shift", "batch")),
        ),
        check_vma=False,
    )
```

profile of v0, /device:TPU:0, one launch (start us, length us, event | category | flops | bytes accessed | tf_op | source)
XLA Modules:
  0.0 146.6 jit_solution(9095668395752551022)
XLA Ops:
  7.2 0.0 reduce-scatter.3.cloned.1.call-start
  7.2 0.0 copy-start
  7.2 2.9 %convert_bitcast_fusion.1 = bf16[768,768]{1,0:T(8,128)(2,1)} fusion(f32[1,768,768]{2,1,0:T(8,128)} %param.12), kind=kLoop, calls=%fused_computation.1 | loop fusion | flops 589824 | bytes 3538944 | tf_op jit(solution)/shard_map/convert_element_type | solution.py:26
  10.2 0.0 reduce-scatter.3.cloned.1.call-update
  10.2 0.0 reduce-scatter.5.cloned.1.call-start
  10.3 0.0 copy-done
  10.3 1.5 %copy.24 = bf16[1,768,768]{1,2,0:T(8,128)(2,1)} copy(f32[1,768,768]{2,1,0:T(8,128)S(1)} %copy-done) | data formatting | bytes 3538944 | tf_op args[1]
  11.7 0.0 copy-start.2
  11.7 0.0 copy-start.3
  11.8 0.0 reduce-scatter.5.cloned.1.call-update
  11.8 0.0 copy-start.4
  11.8 0.0 copy-start.5
  11.8 0.0 all-gather.3.cloned.1.call-start
  11.8 31.1 %reduce-scatter.3.cloned.1.call-done = bf16[192,768]{1,0:T(8,128)(2,1)} async-done(((bf16[768,768]{1,0:T(8,128)(2,1)}), bf16[192,768]{1,0:T(8,128)(2,1)}) %reduce-scatter.3.cloned.1.call-update) | async-done | bytes 294928 | tf_op jit(solution)/shard_map/reduce_scatter | solution.py:25
  42.9 0.0 copy-done.2
  42.9 0.0 copy-done.3
  43.0 2.2 %fusion.3 = (bf16[192,768]{1,0:T(8,128)(2,1)}, f32[192,768]{1,0:T(8,128)}, f32[192,768]{1,0:T(8,128)}) fusion(f32[192,768]{1,0:T(8,128)S(1)} %copy-done.2, bf16[192,768]{1,0:T(8,128)(2,1)} %reduce-scatter.3.cloned.1.call-done, f32[192,768]{1,0:T(8,128)S(1)} %copy-done.3), kind=kLoop, calls=%fused_computation.13 | loop fusion | flops 1032192 | bytes 2949120 | tf_op jit(solution)/shard_map/convert_element_type | solution.py:54
  45.1 0.0 all-gather.3.cloned.1.call-update
  45.2 0.0 copy-start.6
  45.2 0.0 copy-start.7
  45.2 0.0 copy-start.12
  45.2 0.0 copy-start.8
  45.2 0.0 copy-start.9
  45.2 0.0 copy-start.10
  45.2 0.0 copy-start.11
  45.3 0.0 all-gather.5.cloned.1.call-start
  45.3 28.5 %reduce-scatter.5.cloned.1.call-done = bf16[768,192]{0,1:T(8,128)(2,1)} async-done(((bf16[768,768]{0,1:T(8,128)(2,1)}), bf16[768,192]{0,1:T(8,128)(2,1)}) %reduce-scatter.5.cloned.1.call-update) | async-done | bytes 294928 | tf_op jit(solution)/shard_map/reduce_scatter | solution.py:28
  73.8 0.0 copy-done.4
  73.8 0.0 copy-done.5
  73.8 2.2 %fusion.2 = (bf16[768,192]{0,1:T(8,128)(2,1)}, f32[768,192]{0,1:T(8,128)}, f32[768,192]{0,1:T(8,128)}) fusion(f32[768,192]{0,1:T(8,128)S(1)} %copy-done.4, bf16[768,192]{0,1:T(8,128)(2,1)} %reduce-scatter.5.cloned.1.call-done, f32[768,192]{0,1:T(8,128)S(1)} %copy-done.5), kind=kLoop, calls=%fused_computation.12 | loop fusion | flops 1032192 | bytes 2949120 | tf_op jit(solution)/shard_map/convert_element_type | solution.py:55
  76.0 0.0 all-gather.5.cloned.1.call-update
  76.0 0.0 copy-done.6
  76.1 0.0 copy-done.7
  76.1 0.0 copy-done.12
  76.1 0.6 dynamic-slice
  77.3 9.6 %all-reduce.2 = (f32[768]{0:T(1024)S(1)}, f32[768]{0:T(1024)S(1)}) all-reduce(f32[768]{0:T(1024)S(1)} %reduce, f32[768]{0:T(1024)S(1)} %reduce.1), channel_id=1, replica_groups=mesh['shift'=2,'batch'=4,'cols'=4] {'batch'}, use_global_device_ids=true, to_apply=%region_2.0 | all-reduce | flops 1536 | bytes 12288 | tf_op jit(solution)/shard_map/psum | solution.py:32
  87.0 0.0 copy-done.8
  87.0 0.0 copy-done.9
  87.0 0.0 copy-done.10
  87.0 0.0 copy-done.11
  87.0 0.7 fusion
  87.7 0.2 dynamic-update-slice
  87.9 0.2 dynamic-update-slice.1
  88.1 10.7 %all-reduce.3 = (bf16[768]{0:T(1024)(128)(2,1)}, bf16[768]{0:T(1024)(128)(2,1)}) all-reduce(bf16[768]{0:T(1024)(128)(2,1)S(1)} %dynamic-update-slice, bf16[768]{0:T(1024)(128)(2,1)S(1)} %dynamic-update-slice.1), channel_id=1, replica_groups=mesh['shift'=2,'batch'=4,'cols'=4] {'batch'}, use_global_device_ids=true, to_apply=%add | all-reduce | flops 1536 | bytes 6144
  98.7 6.6 %all-gather.3.cloned.1.call-done = bf16[768,768]{1,0:T(8,128)(2,1)} async-done(((bf16[192,768]{1,0:T(8,128)(2,1)}), bf16[768,768]{1,0:T(8,128)(2,1)}) %all-gather.3.cloned.1.call-update) | async-done | bytes 1179664 | tf_op jit(solution)/shard_map/all_gather | solution.py:54
  105.3 0.0 copy-start.1
  105.3 31.4 %all-gather.5.cloned.1.call-done = bf16[768,768]{0,1:T(8,128)(2,1)} async-done(((bf16[768,192]{0,1:T(8,128)(2,1)}), bf16[768,768]{0,1:T(8,128)(2,1)}) %all-gather.5.cloned.1.call-update) | async-done | bytes 1179664 | tf_op jit(solution)/shard_map/all_gather | solution.py:55
  136.7 2.4 %copy.25 = bf16[768,768]{1,0:T(8,128)(2,1)} copy(bf16[768,768]{0,1:T(8,128)(2,1)} %all-gather.5.cloned.1.call-done) | data formatting | bytes 2359296
  139.1 0.0 copy-done.1
  139.1 1.0 copy.29
  (4 shorter events, 0.0 us)
Async XLA Ops:
  7.2 35.8 %reduce-scatter.3.cloned.1.call-start = ((), (), s32[]{:S(2)}) async-start(), calls=%async_computation.2 | async-start | bytes 1474560 | tf_op jit(solution)/shard_map/reduce_scatter | solution.py:25
  7.2 3.0 %copy-start = (f32[1,768,768]{2,1,0:T(8,128)S(1)}, f32[1,768,768]{2,1,0:T(8,128)}, u32[]{:S(2)}) copy-start(f32[1,768,768]{2,1,0:T(8,128)} %param.13) | copy-start | bytes 7077892
  10.2 63.6 %reduce-scatter.5.cloned.1.call-start = ((), (), s32[]{:S(2)}) async-start(), calls=%async_computation.4 | async-start | bytes 1474560 | tf_op jit(solution)/shard_map/reduce_scatter | solution.py:28
  11.7 31.2 %copy-start.2 = (f32[192,768]{1,0:T(8,128)S(1)}, f32[192,768]{1,0:T(8,128)}, u32[]{:S(2)}) copy-start(f32[192,768]{1,0:T(8,128)} %param.16) | copy-start | bytes 1769476
  11.7 31.2 %copy-start.3 = (f32[192,768]{1,0:T(8,128)S(1)}, f32[192,768]{1,0:T(8,128)}, u32[]{:S(2)}) copy-start(f32[192,768]{1,0:T(8,128)} %param.20) | copy-start | bytes 1769476
  11.8 62.0 %copy-start.4 = (f32[768,192]{0,1:T(8,128)S(1)}, f32[768,192]{0,1:T(8,128)}, u32[]{:S(2)}) copy-start(f32[768,192]{0,1:T(8,128)} %param.17) | copy-start | bytes 1769476
  11.8 62.0 %copy-start.5 = (f32[768,192]{0,1:T(8,128)S(1)}, f32[768,192]{0,1:T(8,128)}, u32[]{:S(2)}) copy-start(f32[768,192]{0,1:T(8,128)} %param.21) | copy-start | bytes 1769476
  11.8 93.5 %all-gather.3.cloned.1.call-start = ((), (), s32[]{:S(2)}) async-start(), calls=%async_computation.3 | async-start | bytes 1474560 | tf_op jit(solution)/shard_map/all_gather | solution.py:54
  45.2 30.9 %copy-start.6 = (f32[1,768]{1,0:T(1,128)S(1)}, f32[1,768]{1,0:T(1,128)}, u32[]{:S(2)}) copy-start(f32[1,768]{1,0:T(1,128)} %param.14) | copy-start | bytes 9220
  45.2 30.9 %copy-start.7 = (f32[1,768]{1,0:T(1,128)S(1)}, f32[1,768]{1,0:T(1,128)}, u32[]{:S(2)}) copy-start(f32[1,768]{1,0:T(1,128)} %param.15) | copy-start | bytes 9220
  45.2 30.9 %copy-start.12 = (u32[32]{0:T(128)S(1)}, u32[32]{0:T(128)}, u32[]{:S(2)}) copy-start(u32[32]{0:T(128)} %constant.29) | copy-start | bytes 388
  45.2 41.8 %copy-start.8 = (f32[192]{0:T(256)S(1)}, f32[192]{0:T(256)}, u32[]{:S(2)}) copy-start(f32[192]{0:T(256)} %param.19) | copy-start | bytes 2308
  45.2 41.8 %copy-start.9 = (f32[192]{0:T(256)S(1)}, f32[192]{0:T(256)}, u32[]{:S(2)}) copy-start(f32[192]{0:T(256)} %param.23) | copy-start | bytes 2308
  45.2 41.8 %copy-start.10 = (f32[192]{0:T(256)S(1)}, f32[192]{0:T(256)}, u32[]{:S(2)}) copy-start(f32[192]{0:T(256)} %param.18) | copy-start | bytes 2308
  45.2 41.8 %copy-start.11 = (f32[192]{0:T(256)S(1)}, f32[192]{0:T(256)}, u32[]{:S(2)}) copy-start(f32[192]{0:T(256)} %param.22) | copy-start | bytes 2308
  45.3 91.5 %all-gather.5.cloned.1.call-start = ((), (), s32[]{:S(2)}) async-start(), calls=%async_computation.5 | async-start | bytes 1474560 | tf_op jit(solution)/shard_map/all_gather | solution.py:55
  105.3 33.8 %copy-start.1 = (bf16[768,768]{1,0:T(8,128)(2,1)S(1)}, bf16[768,768]{1,0:T(8,128)(2,1)}, u32[]{:S(2)}) copy-start(bf16[768,768]{1,0:T(8,128)(2,1)} %all-gather.3.cloned.1.call-done) | copy-start | bytes 3538948
Sparse Core Ops, SparseCore 0:
  10.9 32.0 reduce-scatter.2
  45.8 27.9 reduce-scatter.4
  75.9 29.3 all-gather.2
  107.3 29.3 all-gather.4
where the time goes:
time: 147 us
  waiting for transfers between devices  97.6 us (66%)
  blocking collectives  20.3 us (14%)
  between operations  14.6 us (10%)
  other arithmetic  8.02 us (5%)
  local copies, waits for them, and re-layouts  5.93 us (4%)
    all_gather x1, waiting for transfers between devices, on_device(): lax.all_gather(stepped_down.astype(jnp.bfloat16), 'batch', axis=1, tiled=...  31.4 us
    reduce_scatter x1, waiting for transfers between devices, on_device(): lax.psum_scatter(partial_up[0].astype(jnp.bfloat16), 'batch', scatter_dim...  31.1 us
    reduce_scatter x1, waiting for transfers between devices, on_device(): lax.psum_scatter(partial_down[0].astype(jnp.bfloat16), 'batch', scatter_d...  28.5 us
    unnamed x1, blocking collectives  10.7 us
    psum x1, blocking collectives, on_device(): lax.psum((partial_norm[0], partial_bias[0]), 'batch')  9.62 us
    all_gather x1, waiting for transfers between devices, on_device(): lax.all_gather(stepped_up.astype(jnp.bfloat16), 'batch', axis=0, tiled=True)  6.57 us
    unnamed x34, local copies, waits for them, and re-layouts  5.93 us
    convert_element_type x1, other arithmetic, on_device(): partial_up[0].astype(jnp.bfloat16)  2.94 us
  transfers between devices with their start and end apart: 4, of which 4 were waited for; matrix products, arithmetic and copies ran while one was open for 5% of the time, Pallas kernels for 0%

commit v1 on v0

--- a/solution.py
+++ b/solution.py
@@ -1,3 +1,4 @@
+import functools
 import jax
 import jax.numpy as jnp
 from jax import lax
@@ -5,6 +6,14 @@
 
 learn_rate = 0.1
 hold_rate = 0.8
+
+
+def work_rows(x_part, link_axis, in_dim):
+    field_out = jnp.concatenate(lax.all_gather(x_part, axis_name=link_axis), axis=in_dim)
+    return field_out
+
+
+test_flows = functools.partial(work_rows, link_axis="batch", in_dim=1)
 
 
 def on_device(
@@ -52,7 +61,7 @@
     stepped_bias = master_bias - learn_rate * state_new_bias
     compute_up, compute_down, compute_norm, compute_bias = (
         lax.all_gather(stepped_up.astype(jnp.bfloat16), "batch", axis=0, tiled=True),
-        lax.all_gather(stepped_down.astype(jnp.bfloat16), "batch", axis=1, tiled=True),
+        test_flows(stepped_down.astype(jnp.bfloat16)),
         lax.all_gather(stepped_norm.astype(jnp.bfloat16), "batch", axis=0, tiled=True),
         lax.all_gather(stepped_bias.astype(jnp.bfloat16), "batch", axis=0, tiled=True),
     )

time: 147 us -> 145 us (0.986)
  waiting for transfers between devices: 97.6 us -> 93 us
  local copies, waits for them, and re-layouts: 5.93 us -> 10.5 us
  other arithmetic: 8.02 us -> 6.2 us
    all_gather x1, waiting for transfers between devices: 31.4 us -> 5.67 us  [work_rows(): lax.all_gather(x_part, axis_name=link_axis)]
    all_gather x1, waiting for transfers between devices: 6.57 us -> 27.2 us  [on_device(): lax.all_gather(stepped_up.astype(jnp.bfloat16), 'batch', axis=0, tiled=True)]
    reduce_scatter x1, waiting for transfers between devices: 28.5 us -> 31.6 us  [on_device(): lax.psum_scatter(partial_down[0].astype(jnp.bfloat16), 'batch', scatter_d...]
    all_gather x0 -> x1, local copies, waits for them, and re-layouts: none -> 2.7 us  [work_rows(): lax.all_gather(x_part, axis_name=link_axis)]
    reduce_scatter x1, waiting for transfers between devices: 31.1 us -> 28.5 us  [on_device(): lax.psum_scatter(partial_up[0].astype(jnp.bfloat16), 'batch', scatter_dim...]
    convert_element_type x1, other arithmetic: 2.94 us -> 1.13 us  [on_device(): partial_up[0].astype(jnp.bfloat16)]
    unnamed x34 -> x32, local copies, waits for them, and re-layouts: 5.93 us -> 7.7 us
  transfers between devices with their start and end apart: 4 -> 4, of which waited for: 4 -> 4; matrix products, arithmetic and copies ran while one was open for 5% -> 8% of each run, Pallas kernels for 0% -> 0%
where the time goes in v1:
time: 145 us
  waiting for transfers between devices  93 us (64%)
  blocking collectives  20.5 us (14%)
  between operations  14.6 us (10%)
  local copies, waits for them, and re-layouts  10.5 us (7%)
  other arithmetic  6.2 us (4%)
    reduce_scatter x1, waiting for transfers between devices, on_device(): lax.psum_scatter(partial_down[0].astype(jnp.bfloat16), 'batch', scatter_d...  31.6 us
    reduce_scatter x1, waiting for transfers between devices, on_device(): lax.psum_scatter(partial_up[0].astype(jnp.bfloat16), 'batch', scatter_dim...  28.5 us
    all_gather x1, waiting for transfers between devices, on_device(): lax.all_gather(stepped_up.astype(jnp.bfloat16), 'batch', axis=0, tiled=True)  27.2 us
    unnamed x1, blocking collectives  10.9 us
    psum x1, blocking collectives, on_device(): lax.psum((partial_norm[0], partial_bias[0]), 'batch')  9.62 us
    unnamed x32, local copies, waits for them, and re-layouts  7.7 us
    all_gather x1, waiting for transfers between devices, work_rows(): lax.all_gather(x_part, axis_name=link_axis)  5.67 us
  transfers between devices with their start and end apart: 4, of which 4 were waited for; matrix products, arithmetic and copies ran while one was open for 8% of the time, Pallas kernels for 0%

profile of v1, /device:TPU:0, one launch (start us, length us, event | category | flops | bytes accessed | tf_op | source)
XLA Modules:
  0.0 145.0 jit_solution(15452401014706036250)
XLA Ops:
  7.2 0.0 reduce-scatter.5.cloned.1.call-start
  7.2 0.0 copy-start
  7.2 2.8 %copy.28 = bf16[1,768,768]{1,2,0:T(8,128)(2,1)} copy(f32[1,768,768]{2,1,0:T(8,128)} %param.13) | data formatting | bytes 3538944 | tf_op args[1]
  10.1 0.0 reduce-scatter.5.cloned.1.call-update
  10.1 0.0 reduce-scatter.3.cloned.1.call-start
  10.1 0.0 copy-done
  10.2 1.1 convert_bitcast_fusion.1
  11.3 0.0 copy-start.1
  11.3 0.0 copy-start.2
  11.3 0.0 reduce-scatter.3.cloned.1.call-update
  11.3 0.0 copy-start.3
  11.3 0.0 copy-start.4
  11.3 0.0 all-gather.6.cloned.1.call-start
  11.4 31.6 %reduce-scatter.5.cloned.1.call-done = bf16[768,192]{0,1:T(8,128)(2,1)} async-done(((bf16[768,768]{0,1:T(8,128)(2,1)}), bf16[768,192]{0,1:T(8,128)(2,1)}) %reduce-scatter.5.cloned.1.call-update) | async-done | bytes 294928 | tf_op jit(solution)/shard_map/reduce_scatter | solution.py:37
  42.9 0.0 copy-done.1
  42.9 0.0 copy-done.2
  42.9 2.2 %fusion.2 = (bf16[768,192]{0,1:T(8,128)(2,1)}, f32[768,192]{0,1:T(8,128)}, f32[768,192]{0,1:T(8,128)}) fusion(f32[768,192]{0,1:T(8,128)S(1)} %copy-done.1, bf16[768,192]{0,1:T(8,128)(2,1)} %reduce-scatter.5.cloned.1.call-done, f32[768,192]{0,1:T(8,128)S(1)} %copy-done.2), kind=kLoop, calls=%fused_computation.12 | loop fusion | flops 1032192 | bytes 2949120 | tf_op jit(solution)/shard_map/convert_element_type | solution.py:64
  45.1 0.0 all-gather.6.cloned.1.call-update
  45.2 0.0 copy-start.5
  45.2 0.0 copy-start.6
  45.2 0.0 copy-start.11
  45.2 0.0 copy-start.7
  45.2 0.0 copy-start.8
  45.2 0.0 copy-start.9
  45.2 0.0 copy-start.10
  45.2 0.0 all-gather.4.cloned.1.call-start
  45.3 28.5 %reduce-scatter.3.cloned.1.call-done = bf16[192,768]{1,0:T(8,128)(2,1)} async-done(((bf16[768,768]{1,0:T(8,128)(2,1)}), bf16[192,768]{1,0:T(8,128)(2,1)}) %reduce-scatter.3.cloned.1.call-update) | async-done | bytes 294928 | tf_op jit(solution)/shard_map/reduce_scatter | solution.py:34
  73.8 0.0 copy-done.3
  73.8 0.0 copy-done.4
  73.8 2.2 %fusion.3 = (bf16[192,768]{1,0:T(8,128)(2,1)}, f32[192,768]{1,0:T(8,128)}, f32[192,768]{1,0:T(8,128)}) fusion(f32[192,768]{1,0:T(8,128)S(1)} %copy-done.3, bf16[192,768]{1,0:T(8,128)(2,1)} %reduce-scatter.3.cloned.1.call-done, f32[192,768]{1,0:T(8,128)S(1)} %copy-done.4), kind=kLoop, calls=%fused_computation.13 | loop fusion | flops 1032192 | bytes 2949120 | tf_op jit(solution)/shard_map/convert_element_type | solution.py:63
  76.0 0.0 all-gather.4.cloned.1.call-update
  76.0 0.0 copy-done.5
  76.1 0.0 copy-done.6
  76.1 0.0 copy-done.11
  76.1 0.6 dynamic-slice
  77.3 9.6 %all-reduce.2 = (f32[768]{0:T(1024)S(1)}, f32[768]{0:T(1024)S(1)}) all-reduce(f32[768]{0:T(1024)S(1)} %reduce, f32[768]{0:T(1024)S(1)} %reduce.1), channel_id=1, replica_groups=mesh['shift'=2,'batch'=4,'cols'=4] {'batch'}, use_global_device_ids=true, to_apply=%region_2.0 | all-reduce | flops 1536 | bytes 12288 | tf_op jit(solution)/shard_map/psum | solution.py:41
  87.0 0.0 copy-done.7
  87.0 0.0 copy-done.8
  87.0 0.0 copy-done.9
  87.0 0.0 copy-done.10
  87.0 0.7 fusion
  87.7 0.2 dynamic-update-slice
  87.9 0.2 dynamic-update-slice.1
  88.1 10.9 %all-reduce.3 = (bf16[768]{0:T(1024)(128)(2,1)}, bf16[768]{0:T(1024)(128)(2,1)}) all-reduce(bf16[768]{0:T(1024)(128)(2,1)S(1)} %dynamic-update-slice, bf16[768]{0:T(1024)(128)(2,1)S(1)} %dynamic-update-slice.1), channel_id=1, replica_groups=mesh['shift'=2,'batch'=4,'cols'=4] {'batch'}, use_global_device_ids=true, to_apply=%add | all-reduce | flops 1536 | bytes 6144
  99.0 5.7 %all-gather.6.cloned.1.call-done = bf16[3072,192]{0,1:T(8,128)(2,1)} async-done(((bf16[768,192]{0,1:T(8,128)(2,1)}), bf16[3072,192]{0,1:T(8,128)(2,1)}) %all-gather.6.cloned.1.call-update) | async-done | bytes 1179664 | tf_op jit(solution)/shard_map/all_gather | solution.py:12
  104.6 2.7 %reshape.34 = bf16[4,768,192]{1,0,2:T(4,128)(2,1)S(1)} reshape(bf16[3072,192]{0,1:T(8,128)(2,1)} %all-gather.6.cloned.1.call-done) | data formatting | bytes 2359296 | tf_op jit(solution)/shard_map/all_gather | solution.py:12
  107.3 0.1 copy.29
  107.5 1.5 %copy.30 = bf16[768,768]{1,0:T(8,128)(2,1)} copy(bf16[768,768]{0,1:T(8,128)(2,1)S(1)} %bitcast.12) | data formatting | bytes 2359296
  108.9 27.2 %all-gather.4.cloned.1.call-done = bf16[768,768]{1,0:T(8,128)(2,1)} async-done(((bf16[192,768]{1,0:T(8,128)(2,1)}), bf16[768,768]{1,0:T(8,128)(2,1)}) %all-gather.4.cloned.1.call-update) | async-done | bytes 1179664 | tf_op jit(solution)/shard_map/all_gather | solution.py:63
  136.1 2.4 %copy.34 = bf16[768,768]{1,0:T(8,128)(2,1)} copy(bf16[768,768]{1,0:T(8,128)(2,1)} %all-gather.4.cloned.1.call-done) | data formatting | bytes 2359296
  (4 shorter events, 0.0 us)
Async XLA Ops:
  7.2 35.8 %reduce-scatter.5.cloned.1.call-start = ((), (), s32[]{:S(2)}) async-start(), calls=%async_computation.4 | async-start | bytes 1474560 | tf_op jit(solution)/shard_map/reduce_scatter | solution.py:37
  7.2 2.9 %copy-start = (f32[1,768,768]{2,1,0:T(8,128)S(1)}, f32[1,768,768]{2,1,0:T(8,128)}, u32[]{:S(2)}) copy-start(f32[1,768,768]{2,1,0:T(8,128)} %param.12) | copy-start | bytes 7077892
  10.1 63.7 %reduce-scatter.3.cloned.1.call-start = ((), (), s32[]{:S(2)}) async-start(), calls=%async_computation.2 | async-start | bytes 1474560 | tf_op jit(solution)/shard_map/reduce_scatter | solution.py:34
  11.3 31.7 %copy-start.1 = (f32[768,192]{0,1:T(8,128)S(1)}, f32[768,192]{0,1:T(8,128)}, u32[]{:S(2)}) copy-start(f32[768,192]{0,1:T(8,128)} %param.17) | copy-start | bytes 1769476
  11.3 31.7 %copy-start.2 = (f32[768,192]{0,1:T(8,128)S(1)}, f32[768,192]{0,1:T(8,128)}, u32[]{:S(2)}) copy-start(f32[768,192]{0,1:T(8,128)} %param.21) | copy-start | bytes 1769476
  11.3 62.5 %copy-start.3 = (f32[192,768]{1,0:T(8,128)S(1)}, f32[192,768]{1,0:T(8,128)}, u32[]{:S(2)}) copy-start(f32[192,768]{1,0:T(8,128)} %param.16) | copy-start | bytes 1769476
  11.3 62.5 %copy-start.4 = (f32[192,768]{1,0:T(8,128)S(1)}, f32[192,768]{1,0:T(8,128)}, u32[]{:S(2)}) copy-start(f32[192,768]{1,0:T(8,128)} %param.20) | copy-start | bytes 1769476
  11.3 93.3 %all-gather.6.cloned.1.call-start = ((), (), s32[]{:S(2)}) async-start(), calls=%async_computation.5 | async-start | bytes 1474560 | tf_op jit(solution)/shard_map/all_gather | solution.py:12
  45.2 30.9 %copy-start.5 = (f32[1,768]{1,0:T(1,128)S(1)}, f32[1,768]{1,0:T(1,128)}, u32[]{:S(2)}) copy-start(f32[1,768]{1,0:T(1,128)} %param.14) | copy-start | bytes 9220
  45.2 30.9 %copy-start.6 = (f32[1,768]{1,0:T(1,128)S(1)}, f32[1,768]{1,0:T(1,128)}, u32[]{:S(2)}) copy-start(f32[1,768]{1,0:T(1,128)} %param.15) | copy-start | bytes 9220
  45.2 30.9 %copy-start.11 = (u32[32]{0:T(128)S(1)}, u32[32]{0:T(128)}, u32[]{:S(2)}) copy-start(u32[32]{0:T(128)} %constant.29) | copy-start | bytes 388
  45.2 41.8 %copy-start.7 = (f32[192]{0:T(256)S(1)}, f32[192]{0:T(256)}, u32[]{:S(2)}) copy-start(f32[192]{0:T(256)} %param.19) | copy-start | bytes 2308
  45.2 41.8 %copy-start.8 = (f32[192]{0:T(256)S(1)}, f32[192]{0:T(256)}, u32[]{:S(2)}) copy-start(f32[192]{0:T(256)} %param.23) | copy-start | bytes 2308
  45.2 41.8 %copy-start.9 = (f32[192]{0:T(256)S(1)}, f32[192]{0:T(256)}, u32[]{:S(2)}) copy-start(f32[192]{0:T(256)} %param.18) | copy-start | bytes 2308
  45.2 41.8 %copy-start.10 = (f32[192]{0:T(256)S(1)}, f32[192]{0:T(256)}, u32[]{:S(2)}) copy-start(f32[192]{0:T(256)} %param.22) | copy-start | bytes 2308
  45.2 90.9 %all-gather.4.cloned.1.call-start = ((), (), s32[]{:S(2)}) async-start(), calls=%async_computation.3 | async-start | bytes 1474560 | tf_op jit(solution)/shard_map/all_gather | solution.py:63
Sparse Core Ops, SparseCore 0:
  10.9 32.0 reduce-scatter.4
  45.8 27.9 reduce-scatter.2
  75.4 29.2 all-gather.5
  106.6 29.4 all-gather.3
